TPU v7x, 32 devices: a whole 2x2x4 slice. The times are simulated.
32 devices in a mesh: seq: 8 (over z, core), cp: 4 (over y, x).
Axes of the slice: x: 2, y: 2, z: 4, core: 2. Of those that a mesh axis runs over, the one named last changes fastest.
Arguments:
- queries: bfloat16 [4096, 768], P(('seq', 'cp')), parts along dimension 0, may hold values from -6 to 6, as said below
- keys: bfloat16 [4096, 128], P(('seq', 'cp')), parts along dimension 0, may hold values from -6 to 6, as said below
- values: bfloat16 [4096, 128], P(('seq', 'cp')), parts along dimension 0, may hold values from -6 to 6
- out_grad: bfloat16 [4096, 768], P(('seq', 'cp')), parts along dimension 0, may hold values from -6 to 6
- positions: int32 [3, 4096], P(None, 'seq'), parts along dimension 1, may hold values from 0 to 511
- doc_ids: int32 [4096], P('seq'), parts along dimension 0, may hold values from 0 to 7, never falling along the last dimension, each value on 1 to 256 neighbouring positions
- stretch_order: int32 [64], P('seq'), parts along dimension 0, may hold values from 0 to 7, each once
Outputs:
- attn_out: bfloat16 [4096, 768], P(('seq', 'cp')), parts along dimension 0
- grad_queries: bfloat16 [4096, 768], P(('seq', 'cp')), parts along dimension 0
- grad_keys: bfloat16 [4096, 128], P(('seq', 'cp')), parts along dimension 0
- grad_values: bfloat16 [4096, 128], P(('seq', 'cp')), parts along dimension 0
There are 8 independent parts, one for each index of `seq`. A program takes and returns all parts, laid end to end along the dimension named above; each array names one. Nothing has to cross between parts.
Inputs may be any that keep to these rules, and one draw needn't show every extreme that they name: `queries`: values of one part; a few tokens may have large entries. `keys`: values of one part; a few tokens may have large entries. `doc_ids`: never falls along the sequence; each document holds at most 256 tokens. `stretch_order`: each block number appears once.
All inputs are finite; a program needn't handle non-finite values.
Results may differ from a plain program's by a relative error of at most 0.01.
Values may be sent and summed in bfloat16 or wider, within the bound.
A program may use at most 64 MiB of HBM per device.

v0:
```python
import math

import jax
import jax.numpy as jnp
from jax import lax
from jax.sharding import PartitionSpec as P

HQ = 6
HK = 1
HD = 128
SEC_T = 16
SEC_H = 24


def rotary_tables(pos3):
    half = HD // 2
    pairs = jnp.arange(half, dtype=jnp.int32)
    freqs = jnp.exp(-(2.0 * pairs.astype(jnp.float32) / HD) * math.log(1000000.0))
    pos_f = pos3.astype(jnp.float32)
    chosen = jnp.where(
        (pairs < SEC_T)[None, :],
        pos_f[0][:, None],
        jnp.where((pairs < SEC_T + SEC_H)[None, :], pos_f[1][:, None], pos_f[2][:, None]),
    )
    angle = chosen * freqs[None, :]
    cosine = jnp.concatenate([jnp.cos(angle), jnp.cos(angle)], axis=1)
    sine_tab = jnp.concatenate([jnp.sin(angle), jnp.sin(angle)], axis=1)
    return (cosine, sine_tab)


def rotate(field, cosine, sine_tab):
    half = HD // 2
    first, second = (field[..., :half], field[..., half:])
    turned = jnp.concatenate([-second, first], axis=-1)
    return field * cosine[:, None, :] + turned * sine_tab[:, None, :]


def rotate_back(field, cosine, sine_tab):
    half = HD // 2
    scaled = field * sine_tab[:, None, :]
    turned = jnp.concatenate([scaled[..., half:], -scaled[..., :half]], axis=-1)
    return field * cosine[:, None, :] + turned


def dot_nt(left, right):
    return lax.dot_general(
        left, right, (((1,), (1,)), ((), ())), preferred_element_type=jnp.float32
    )


def dot_tn(left, right):
    return lax.dot_general(
        left, right, (((0,), (0,)), ((), ())), preferred_element_type=jnp.float32
    )


def score_products(left, right):
    return dot_nt(left, right)


def weighted_rows(weights, right):
    return jnp.dot(weights, right, preferred_element_type=jnp.float32)


def shards(queries, keys, values, out_grad, positions, doc_ids, stretch_order):
    devices = lax.axis_size("cp")
    my_rank = lax.axis_index("cp")
    tok_rows = queries.shape[0]
    half_len = tok_rows // 2
    total = tok_rows * devices
    group_size = HQ // HK
    score_scale = 1.0 / math.sqrt(HD)
    within = jnp.arange(half_len, dtype=jnp.int32)
    order_all = (stretch_order[:, None] * half_len + within[None, :]).reshape(total)
    orig_local = lax.dynamic_slice_in_dim(order_all, my_rank * tok_rows, tok_rows)
    doc_all = doc_ids[order_all]
    doc_local = doc_ids[orig_local]
    cosine, sine_tab = rotary_tables(positions[:, orig_local])
    q_rot = rotate(queries.astype(jnp.float32).reshape(tok_rows, HQ, HD), cosine, sine_tab).astype(
        jnp.bfloat16
    )
    k_rot = rotate(keys.astype(jnp.float32).reshape(tok_rows, HK, HD), cosine, sine_tab).astype(
        jnp.bfloat16
    )
    k_flat = k_rot.reshape(tok_rows, HK * HD)
    keys_all, values_all = (
        lax.all_gather(k_flat, "cp", axis=0, tiled=True),
        lax.all_gather(values, "cp", axis=0, tiled=True),
    )
    allowed = (doc_local[:, None] == doc_all[None, :]) & (order_all[None, :] <= orig_local[:, None])
    mask_rows = jnp.repeat(allowed, group_size, axis=0)
    grad_heads = out_grad.reshape(tok_rows, HQ, HD)
    outputs, dq_list, dscore_list, prob_list, query_list, dout_list, lse_list, delta_list = (
        [],
        [],
        [],
        [],
        [],
        [],
        [],
        [],
    )
    q_grp = q_rot.reshape(tok_rows * group_size, HD)
    do_grp = grad_heads.reshape(tok_rows * group_size, HD)
    scores = score_products(q_grp, keys_all) * score_scale
    scores = jnp.where(mask_rows, scores, -jnp.inf)
    top = jnp.max(scores, axis=-1, keepdims=True)
    expo = jnp.exp(scores - top)
    row_total = jnp.sum(expo, axis=-1, keepdims=True)
    probs32 = expo / row_total
    probs = probs32.astype(jnp.bfloat16)
    outputs.append(weighted_rows(probs, values_all).astype(jnp.bfloat16))
    dprobs = score_products(do_grp, values_all)
    delta = jnp.sum(probs32 * dprobs, axis=-1, keepdims=True)
    dscores = (probs32 * (dprobs - delta)).astype(jnp.bfloat16)
    dq_list.append(
        (weighted_rows(dscores, keys_all) * score_scale).reshape(tok_rows, group_size, HD)
    )
    dscore_list.append(dscores)
    prob_list.append(probs)
    query_list.append(q_grp)
    dout_list.append(do_grp)
    lse_list.append((top + jnp.log(row_total)).reshape(tok_rows, group_size))
    delta_list.append(delta.reshape(tok_rows, group_size))
    attn_out = (
        jnp.stack(outputs, axis=0)
        .reshape(HK, tok_rows, group_size * HD)
        .transpose(1, 0, 2)
        .reshape(tok_rows, HQ * HD)
    )
    dq_rot = dq_list[0]
    pieces = []
    group_id = 0
    part_ds = dscore_list[group_id]
    pieces.append(dot_tn(part_ds, query_list[group_id]) * score_scale)
    group_id = 0
    part_pr = prob_list[group_id]
    pieces.append(dot_tn(part_pr, dout_list[group_id]))
    summed = lax.psum_scatter(
        jnp.concatenate(pieces, axis=1), "cp", scatter_dimension=0, tiled=True
    )
    dk_rot = summed[:, : HK * HD].reshape(tok_rows, HK, HD)
    grad_values = summed[:, HK * HD :].astype(jnp.bfloat16)
    grad_queries = (
        rotate_back(dq_rot, cosine, sine_tab).astype(jnp.bfloat16).reshape(tok_rows, HQ * HD)
    )
    grad_keys = (
        rotate_back(dk_rot, cosine, sine_tab).astype(jnp.bfloat16).reshape(tok_rows, HK * HD)
    )
    return (attn_out, grad_queries, grad_keys, grad_values)


def solution(mesh):
    placed = (
        P(("seq", "cp"), None),
        P(("seq", "cp"), None),
        P(("seq", "cp"), None),
        P(("seq", "cp"), None),
        P(None, "seq"),
        P("seq"),
        P("seq"),
    )
    return jax.shard_map(
        shards,
        mesh=mesh,
        in_specs=placed,
        out_specs=(
            P(("seq", "cp"), None),
            P(("seq", "cp"), None),
            P(("seq", "cp"), None),
            P(("seq", "cp"), None),
        ),
        check_vma=False,
    )
```

profile of v0, /device:TPU:0, one launch (start us, length us, event | category | flops | bytes accessed | tf_op | source)
XLA Modules:
  0.0 75.9 jit_solution(342246391491716321)
XLA Ops:
  7.3 1.1 %copy.17 = bf16[128,768]{0,1:T(8,128)(2,1)S(1)} copy(bf16[128,768]{1,0:T(8,128)(2,1)} %param.7) | data formatting | bytes 393216 | tf_op args[0]
  9.1 0.6 gather_fusion.2
  9.7 0.2 slice_reduce_fusion.2
  10.1 0.2 fusion.14
  10.7 0.2 copy.21
  11.0 0.2 copy.22
  11.4 9.9 %all_gather.6 = bf16[512,128]{0,1:T(8,128)(2,1)S(1)} all-gather(bf16[128,128]{0,1:T(8,128)(2,1)S(1)} %get-tuple-element.25), channel_id=1, replica_groups=mesh['seq'=8,'cp'=4] {'cp'}, dimensions={0}, use_global_device_ids=true | all-gather | bytes 163840 | tf_op jit(solution)/shard_map/all_gather | solution.py:87
  21.3 1.3 %gather_fusion = s32[128]{0:T(128)S(1)} fusion(s32[512]{0:T(512)S(1)} %copy-done, s32[1024]{0:T(1024)S(1)} %pad_clamp_fusion.1), kind=kCustom, calls=%fused_computation | custom fusion | bytes 1536 | tf_op jit(solution)/shard_map/gather | solution.py:77
  22.6 3.5 %gather_fusion.1 = s32[512]{0:T(512)S(1)} fusion(s32[512]{0:T(512)S(1)} %copy-done, s32[1024]{0:T(1024)S(1)} %pad_clamp_fusion), kind=kCustom, calls=%fused_computation.1 | custom fusion | bytes 6144 | tf_op jit(solution)/shard_map/gather | solution.py:76
  26.3 0.2 broadcast_in_dim.78
  26.5 0.3 reshape.124
  26.9 0.5 copy.25
  27.6 8.4 %all_gather.7 = bf16[512,128]{1,0:T(8,128)(2,1)S(1)} all-gather(bf16[128,128]{1,0:T(8,128)(2,1)S(1)} %copy-done.2), channel_id=1, replica_groups=mesh['seq'=8,'cp'=4] {'cp'}, dimensions={0}, use_global_device_ids=true | all-gather | bytes 163840 | tf_op jit(solution)/shard_map/all_gather | solution.py:88
  36.2 0.5 fusion.18
  36.7 0.3 fusion.1
  36.9 0.5 fusion.5
  37.4 0.4 multiply_reduce_fusion
  37.8 0.4 multiply_convert_fusion
  38.2 0.4 convolution_multiply_fusion.1
  38.6 0.8 %pad_maximum_fusion.1 = f32[512,256]{0,1:T(8,128)} fusion(f32[512,128]{0,1:T(8,128)S(1)} %fusion.5, f32[512,128]{0,1:T(8,128)S(1)} %convolution_multiply_fusion.1), kind=kLoop, calls=%fused_computation.14 | loop fusion | flops 131072 | bytes 1048576 | tf_op jit(solution)/shard_map/concatenate | solution.py:140
  39.5 0.4 convolution_multiply_fusion
  40.1 0.2 fusion.17
  40.3 0.2 pad_maximum_fusion
  41.0 0.8 %copy.28 = bf16[128,768]{1,0:T(8,128)(2,1)} copy(bf16[128,768]{0,1:T(8,128)(2,1)S(1)} %fusion.4) | data formatting | bytes 393216
  41.8 0.5 convolution_convert_fusion
  42.3 0.9 %reshape_transpose_reshape_stack.3 = bf16[128,768]{1,0:T(8,128)(2,1)} reshape(bf16[768,128]{1,0:T(8,128)(2,1)S(1)} %convolution_convert_fusion) | data formatting | bytes 393216 | tf_op jit(solution)/shard_map/reshape;transpose;reshape;stack | solution.py:129
  43.1 21.9 %reduce-scatter.2.cloned.1.call-done = f32[128,256]{0,1:T(8,128)} async-done(((f32[512,256]{0,1:T(8,128)}), f32[128,256]{0,1:T(8,128)}) %reduce-scatter.2.cloned.1.call-update) | async-done | bytes 131088 | tf_op jit(solution)/shard_map/reduce_scatter | solution.py:139
  65.0 0.8 %multiply_bitcast_fusion = f32[128,1,128]{0,2,1:T(8,128)S(1)} fusion(f32[128,256]{0,1:T(8,128)} %reduce-scatter.2.cloned.1.call-done, f32[128,64]{0,1:T(8,128)S(1)} %get-tuple-element.29), kind=kLoop, calls=%fused_computation.41 | loop fusion | flops 32768 | bytes 163840 | tf_op jit(solution)/shard_map/mul | solution.py:40
  65.9 0.9 %fusion.10 = bf16[128,128]{0,1:T(8,128)(2,1)S(1)} fusion(f32[128,64]{0,1:T(8,128)S(1)} %get-tuple-element.22, f32[128,64]{0,1:T(8,128)S(1)} %get-tuple-element.21, f32[128,256]{0,1:T(8,128)} %reduce-scatter.2.cloned.1.call-done, f32[128,64]{0,1:T(8,128)S(1)} %get-tuple-element.28), kind=kLoop, calls=%fused_computation.39 | loop fusion | flops 81920 | bytes 196608 | tf_op jit(solution)/shard_map/convert_element_type | solution.py:148
  66.7 0.7 copy.29
  67.5 0.8 %slice.88 = bf16[128,128]{0,1:T(8,128)(2,1)S(1)} slice(f32[128,256]{0,1:T(8,128)} %reduce-scatter.2.cloned.1.call-done), slice={[0:128], [128:256]} | slice | bytes 65536 | tf_op jit(solution)/shard_map/slice | solution.py:143
  68.3 0.7 copy.30
  (52 shorter events, 2.5 us)
Async XLA Ops:
  7.2 14.1 %copy-start = (s32[512]{0:T(512)S(1)}, s32[512]{0:T(512)}, u32[]{:S(2)}) copy-start(s32[512]{0:T(512)} %param.12) | copy-start | bytes 6148
  7.2 1.4 %copy-start.5 = (s32[8]{0:T(128)S(1)}, s32[8]{0:T(128)}, u32[]{:S(2)}) copy-start(s32[8]{0:T(128)} %param.13) | copy-start | bytes 100
  7.2 1.7 %copy-start.4 = (s32[3,512]{1,0:T(4,128)S(1)}, s32[3,512]{1,0:T(4,128)}, u32[]{:S(2)}) copy-start(s32[3,512]{1,0:T(4,128)} %param.11) | copy-start | bytes 18436
  7.2 2.7 %copy-start.3 = (bf16[128,128]{1,0:T(8,128)(2,1)S(1)}, bf16[128,128]{1,0:T(8,128)(2,1)}, u32[]{:S(2)}) copy-start(bf16[128,128]{1,0:T(8,128)(2,1)} %param.8) | copy-start | bytes 98308
  7.2 57.8 %reduce-scatter.2.cloned.1.call-start = ((), (), s32[]{:S(2)}) async-start(), calls=%async_computation.1 | async-start | bytes 655360 | tf_op jit(solution)/shard_map/reduce_scatter | solution.py:139
  26.1 1.2 %copy-start.1 = (bf16[128,768]{1,0:T(8,128)(2,1)S(1)}, bf16[128,768]{1,0:T(8,128)(2,1)}, u32[]{:S(2)}) copy-start(bf16[128,768]{1,0:T(8,128)(2,1)} %param.10) | copy-start | bytes 589828
  26.2 1.4 %copy-start.2 = (bf16[128,128]{1,0:T(8,128)(2,1)S(1)}, bf16[128,128]{1,0:T(8,128)(2,1)}, u32[]{:S(2)}) copy-start(bf16[128,128]{1,0:T(8,128)(2,1)} %param.9) | copy-start | bytes 98308
Sparse Core Ops, SparseCore 0:
  39.6 25.3 reduce-scatter.1
where the time goes:
time: 76.2 us; the launch traced here: 75.9 us
  waiting for transfers between devices  21.9 us (29%)
  blocking collectives  18.4 us (24%)
  between operations  14.5 us (19%)
  local copies, waits for them, and re-layouts  13.9 us (18%)
  other arithmetic  4.53 us (6%)
  matrix products  2.63 us (3%)
    reduce_scatter x1, waiting for transfers between devices, shards(): lax.psum_scatter(jnp.concatenate(pieces, axis=1), 'cp', scatter_dimension...  21.9 us
    all_gather x1, blocking collectives, shards(): lax.all_gather(k_flat, 'cp', axis=0, tiled=True)  9.94 us
    all_gather x1, blocking collectives, shards(): lax.all_gather(values, 'cp', axis=0, tiled=True)  8.44 us
    unnamed x19, local copies, waits for them, and re-layouts  3.74 us
    gather x1, local copies, waits for them, and re-layouts, shards(): doc_all = doc_ids[order_all]  3.51 us
  transfers between devices with their start and end apart: 1, of which 1 were waited for; matrix products, arithmetic and copies ran while one was open for 5% of the time, Pallas kernels for 0%

commit v1 on v0

v1 whole, which is shorter than its diff:
```python
import functools
import math

import jax
import jax.numpy as jnp
from jax import lax
from jax.experimental import pallas as pl
from jax.experimental.pallas import tpu as pltpu
from jax.sharding import PartitionSpec as P

HQ = 6
HD = 128
SEC_T = 16
SEC_H = 24
BASE = 1000000.0
NEG = -1e30
F32 = jnp.float32
BF16 = jnp.bfloat16


def nt(a, b):
    return lax.dot_general(a, b, (((1,), (1,)), ((), ())), preferred_element_type=F32)


def nn(a, b):
    return lax.dot_general(a, b, (((1,), (0,)), ((), ())), preferred_element_type=F32)


def cos_turns(turns):
    r = turns - jnp.round(turns)
    b = 0.25 - jnp.abs(r)
    z = b * b
    acc = None
    for power in (11, 9, 7, 5, 3, 1):
        coef = (-1.0) ** ((power - 1) // 2) * (2.0 * math.pi) ** power / math.factorial(power)
        acc = jnp.full_like(z, coef) if acc is None else acc * z + coef
    return acc * b


def flip(me, i):
    out, bit = me, 1
    while bit <= i:
        if i & bit:
            out = out + bit - 2 * bit * ((me // bit) % 2)
        bit *= 2
    return out


def repeat(n, small, body):
    if small:
        for i in range(n):
            body(i)
    else:
        lax.fori_loop(0, n, lambda i, c: (body(i), c)[1], 0)


def kernel(n, order_ref, q_hbm, k_hbm, v_hbm, do_hbm, pos_hbm, doc_hbm,
           out_ref, gq_ref, gk_ref, gv_ref,
           q_in, do_in, pos_in, doc_in, k_all, v_all, feat, lay, seqtab, q_rot, do_st, krot,
           cos_t, sin_t, s_buf, dp_buf, p_buf, ds_buf, send_buf, recv_buf,
           in_sem, ks_sem, kr_sem, vs_sem, vr_sem, gs_sem, gr_sem):
    me = lax.axis_index("cp")
    rows = k_hbm.shape[0]
    total = rows * n
    stretch = total // order_ref.shape[0]
    per = rows // stretch
    small = n <= 4 and n & (n - 1) == 0
    scale = 1.0 / math.sqrt(HD)
    mine = pl.ds(pl.multiple_of(me * rows, rows), rows)

    def to(i):
        return flip(me, i) if small else lax.rem(me + i, n)

    def frm(i):
        return flip(me, i) if small else lax.rem(me + n - i, n)

    def span(c):
        return pl.ds(pl.multiple_of(c * rows, rows), rows)

    loads = [
        pltpu.make_async_copy(src, dst, in_sem.at[j])
        for j, (src, dst) in enumerate((
            (k_hbm, k_all.at[mine]), (v_hbm, v_all.at[mine]), (pos_hbm, pos_in),
            (doc_hbm, doc_in), (q_hbm, q_in), (do_hbm, do_in)))
    ]
    for cp in loads:
        cp.start()

    barrier = pltpu.get_barrier_semaphore()

    def greet(i):
        pl.semaphore_signal(barrier, inc=1, device_id={"cp": to(i + 1)},
                            device_id_type=pl.DeviceIdType.MESH)

    repeat(n - 1, small, greet)
    loads[0].wait()
    loads[1].wait()
    pl.semaphore_wait(barrier, n - 1)

    def kcopy(i):
        return pltpu.make_async_remote_copy(
            src_ref=k_all.at[mine], dst_ref=k_all.at[mine], send_sem=ks_sem.at[i],
            recv_sem=kr_sem.at[i], device_id={"cp": to(i)}, device_id_type=pl.DeviceIdType.MESH)

    def vcopy(i):
        return pltpu.make_async_remote_copy(
            src_ref=v_all.at[mine], dst_ref=v_all.at[mine], send_sem=vs_sem.at[i],
            recv_sem=vr_sem.at[i], device_id={"cp": to(i)}, device_id_type=pl.DeviceIdType.MESH)

    repeat(n - 1, small, lambda i: kcopy(n - 1 - i).start())
    repeat(n - 1, small, lambda i: vcopy(n - 1 - i).start())

    for j in (2, 3):
        loads[j].wait()
    feat[...] = jnp.zeros_like(feat)
    feat[0:3, :] = pos_in[...].astype(F32)
    feat[3:4, :] = doc_in[...].astype(F32)
    tiles = [feat[:, t * rows:(t + 1) * rows] for t in range(n)]
    moved = [[tiles[t] if k == 0 else pltpu.roll(tiles[t], k * stretch, 1) for k in range(per)]
             for t in range(n)]
    lane8 = lax.broadcasted_iota(jnp.int32, (8, rows), 1)
    for t in range(n):
        whole = None
        for b in range(per):
            want = jnp.full((8, rows), order_ref[t * per + b], jnp.int32)
            acc = moved[0][b]
            for s in range(1, n * per):
                acc = jnp.where(want == s, moved[s // per][(b - s % per) % per], acc)
            whole = acc if b == 0 else jnp.where(lane8 >= b * stretch, acc, whole)
        lay[:, t * rows:(t + 1) * rows] = whole
    lane = lax.broadcasted_iota(jnp.int32, (8, 2 * HD), 1)
    row8 = lax.broadcasted_iota(jnp.int32, (8, 2 * HD), 0)
    pair = lane % (HD // 2)
    section = jnp.where(pair < SEC_T, 0, jnp.where(pair < SEC_T + SEC_H, 1, 2))
    freq = jnp.exp(pair.astype(F32) * (-2.0 / HD * math.log(BASE))) * (0.5 / math.pi)
    weights = jnp.where(lane < HD, jnp.where(row8 == section, freq, 0.0),
                        jnp.where(row8 == 3, 1.0, 0.0))
    seqtab[...] = lax.dot_general(lay[...], weights, (((0,), (0,)), ((), ())),
                                  precision=lax.Precision.HIGHEST, preferred_element_type=F32)

    first = lax.broadcasted_iota(jnp.int32, (rows, HD), 1) < HD // 2

    def blocks(c):
        return seqtab[span(c), :]

    def tables(turns):
        both = cos_turns(jnp.where(first, turns, turns - 0.25))
        other = pltpu.roll(both, HD // 2, 1)
        return jnp.where(first, both, other), jnp.where(first, -other, both)

    def turned(x):
        return pltpu.roll(x, HD // 2, 1)

    own = blocks(me)
    cosine, sine = tables(own[:, :HD])
    cos_t[...] = cosine
    sin_t[...] = sine
    r_idx = lax.broadcasted_iota(jnp.int32, (rows, HD), 0)
    l_idx = lax.broadcasted_iota(jnp.int32, (rows, HD), 1)
    doc_r = lay[3:4, mine]

    def places(c, idx):
        out = idx + order_ref[c * per] * stretch
        for b in range(1, per):
            out = jnp.where(idx >= b * stretch,
                            idx - b * stretch + order_ref[c * per + b] * stretch, out)
        return out

    orig_r = places(me, l_idx)

    loads[4].wait()
    loads[5].wait()
    for h in range(HQ):
        x = q_in[:, h * HD:(h + 1) * HD].astype(F32)
        q_rot[h * rows:(h + 1) * rows, :] = (x * cosine + turned(x) * sine).astype(BF16)
        do_st[h * rows:(h + 1) * rows, :] = do_in[:, h * HD:(h + 1) * HD]

    def chunk(c, tab, cc, ss, top):
        allowed = (tab[:, HD:] == doc_r) & (places(c, r_idx) <= orig_r)
        bias = jnp.where(allowed, 0.0, NEG)
        x = k_all[span(c), :].astype(F32)
        kr = (x * cc + turned(x) * ss).astype(BF16)
        krot[span(c), :] = kr
        sc = nt(kr, q_rot[...])
        tops = []
        for h in range(HQ):
            part = sc[:, h * HD:(h + 1) * HD] + bias
            s_buf[span(c), h * HD:(h + 1) * HD] = part
            tops.append(jnp.max(part, axis=0, keepdims=True))
        return jnp.maximum(top, jnp.concatenate(tops, axis=1))

    def grads(c):
        dp_buf[span(c), :] = nt(v_all[span(c), :], do_st[...])

    top = jnp.full((1, HQ * rows), NEG, F32)
    top = chunk(me, own, cosine, sine, top)
    grads(me)

    def arrive(i, top):
        c = frm(i)
        tab = blocks(c)
        cc, ss = tables(tab[:, :HD])
        kcopy(i).wait_recv()
        top = chunk(c, tab, cc, ss, top)
        vcopy(i).wait_recv()
        grads(c)
        return top

    if small:
        for i in range(1, n):
            top = arrive(i, top)
    else:
        top = lax.fori_loop(1, n, arrive, top)

    factor = scale * math.log2(math.e)

    def soft(c, carry):
        total_p, total_d = carry
        p = jnp.exp2((s_buf[span(c), :] - top) * factor)
        s_buf[span(c), :] = p
        return (total_p + jnp.sum(p, axis=0, keepdims=True),
                total_d + jnp.sum(p * dp_buf[span(c), :], axis=0, keepdims=True))

    zero = jnp.zeros((1, HQ * rows), F32)
    carry = (zero, zero)
    if small:
        for c in range(n):
            carry = soft(c, carry)
    else:
        carry = lax.fori_loop(0, n, soft, carry)
    inv = 1.0 / carry[0]
    delta = carry[1] * inv

    def back(c):
        probs = s_buf[span(c), :] * inv
        pb = probs.astype(BF16)
        db = (probs * (dp_buf[span(c), :] - delta)).astype(BF16)
        p_buf[span(c), :] = pb
        ds_buf[span(c), :] = db
        return nn(db, q_rot[...]) * scale, nn(pb, do_st[...])

    def gcopy(i):
        return pltpu.make_async_remote_copy(
            src_ref=send_buf.at[i - 1], dst_ref=recv_buf.at[i - 1], send_sem=gs_sem.at[i],
            recv_sem=gr_sem.at[i], device_id={"cp": to(i)}, device_id_type=pl.DeviceIdType.MESH)

    def give(j):
        i = n - 1 - j
        dk, dv = back(to(i))
        send_buf[i - 1, :, :HD] = dk.astype(BF16)
        send_buf[i - 1, :, HD:] = dv.astype(BF16)
        gcopy(i).start()

    repeat(n - 1, small, give)
    dk, dv = back(me)

    outt = lax.dot_general(v_all[...], p_buf[...], (((0,), (0,)), ((), ())),
                           preferred_element_type=F32)
    dqt = lax.dot_general(krot[...], ds_buf[...], (((0,), (0,)), ((), ())),
                          preferred_element_type=F32) * scale
    for h in range(HQ):
        cols = slice(h * HD, (h + 1) * HD)
        out_ref[:, cols] = jnp.transpose(outt[:, h * rows:(h + 1) * rows]).astype(BF16)
        y = jnp.transpose(dqt[:, h * rows:(h + 1) * rows])
        gq_ref[:, cols] = (y * cos_t[...] - turned(y) * sin_t[...]).astype(BF16)

    def take(i, carry):
        gcopy(i).wait_recv()
        return (carry[0] + recv_buf[i - 1, :, :HD].astype(F32),
                carry[1] + recv_buf[i - 1, :, HD:].astype(F32))

    if small:
        for i in range(1, n):
            dk, dv = take(i, (dk, dv))
    else:
        dk, dv = lax.fori_loop(1, n, take, (dk, dv))
    gk_ref[...] = (dk * cos_t[...] - turned(dk) * sin_t[...]).astype(BF16)
    gv_ref[...] = dv.astype(BF16)

    def finish(j):
        kcopy(j + 1).wait_send()
        vcopy(j + 1).wait_send()
        gcopy(j + 1).wait_send()

    repeat(n - 1, small, finish)


def write_out(a, b, c, d, a_out, b_out, c_out, d_out, sem):
    copies = [
        pltpu.make_async_copy(src, dst, sem.at[j])
        for j, (src, dst) in enumerate(((a, a_out), (b, b_out), (c, c_out), (d, d_out)))
    ]
    for cp in copies:
        cp.start()
    for cp in copies:
        cp.wait()


def shards(queries, keys, values, out_grad, positions, doc_ids, stretch_order):
    n = lax.axis_size("cp")
    rows = queries.shape[0]
    total = rows * n
    wide = HQ * HD
    hbm = pl.BlockSpec(memory_space=pltpu.HBM)
    vmem = pl.BlockSpec(memory_space=pltpu.VMEM)
    dma = pltpu.SemaphoreType.DMA
    shapes = ((rows, wide), (rows, wide), (rows, HD), (rows, HD))
    held = pl.pallas_call(
        functools.partial(kernel, n),
        out_shape=tuple(pltpu.VMEM(shape, BF16) for shape in shapes),
        in_specs=[pl.BlockSpec(memory_space=pltpu.SMEM)] + [hbm] * 6,
        out_specs=(vmem,) * 4,
        scratch_shapes=[
            pltpu.VMEM((rows, wide), BF16),
            pltpu.VMEM((rows, wide), BF16),
            pltpu.VMEM((3, total), jnp.int32),
            pltpu.VMEM((1, total), jnp.int32),
            pltpu.VMEM((total, HD), BF16),
            pltpu.VMEM((total, HD), BF16),
            pltpu.VMEM((8, total), F32),
            pltpu.VMEM((8, total), F32),
            pltpu.VMEM((total, 2 * HD), F32),
            pltpu.VMEM((HQ * rows, HD), BF16),
            pltpu.VMEM((HQ * rows, HD), BF16),
            pltpu.VMEM((total, HD), BF16),
            pltpu.VMEM((rows, HD), F32),
            pltpu.VMEM((rows, HD), F32),
            pltpu.VMEM((total, HQ * rows), F32),
            pltpu.VMEM((total, HQ * rows), F32),
            pltpu.VMEM((total, HQ * rows), BF16),
            pltpu.VMEM((total, HQ * rows), BF16),
            pltpu.VMEM((n - 1, rows, 2 * HD), BF16),
            pltpu.VMEM((n - 1, rows, 2 * HD), BF16),
            dma((6,)),
            dma((n,)), dma((n,)), dma((n,)), dma((n,)), dma((n,)), dma((n,)),
        ],
        compiler_params=pltpu.CompilerParams(collective_id=0, has_side_effects=True),
    )(stretch_order, queries, keys, values, out_grad, positions, doc_ids[None, :])
    return pl.pallas_call(
        write_out,
        out_shape=tuple(jax.ShapeDtypeStruct(shape, BF16) for shape in shapes),
        in_specs=[vmem] * 4,
        out_specs=(hbm,) * 4,
        scratch_shapes=[dma((4,))],
    )(*[pltpu.with_memory_space_constraint(x, pltpu.VMEM) for x in held])


def solution(mesh):
    split = P(("seq", "cp"), None)
    return jax.shard_map(
        shards,
        mesh=mesh,
        in_specs=(split, split, split, split, P(None, "seq"), P("seq"), P("seq")),
        out_specs=(split, split, split, split),
        check_vma=False,
    )
```

time: 76.2 us -> 17 us (0.22)
  waiting for transfers between devices: 21.9 us -> 0 us
  blocking collectives: 18.4 us -> 0 us
  Pallas kernels: 0 us -> 16.2 us
  local copies, waits for them, and re-layouts: 13.9 us -> 0 us
  between operations: 14.5 us -> 0.64 us
  other arithmetic: 4.53 us -> 0 us
  matrix products: 2.63 us -> 0 us
    reduce_scatter x1 -> x0, waiting for transfers between devices: 21.9 us -> none  [shards(): lax.psum_scatter(jnp.concatenate(pieces, axis=1), 'cp', scatter_dimension...]
    all_gather x2 -> x0, blocking collectives: 18.4 us -> none  [the longest x1 9.94 us: shards(): lax.all_gather(k_flat, 'cp', axis=0, tiled=True)]
    pallas_call x0 -> x2, Pallas kernels: none -> 16.2 us  [the longest x1 15.4 us: shards(): pl.pallas_call(functools.partial(kernel, n), out_shape=tuple((pltpu.VMEM(...]
    gather x3 -> x0, local copies, waits for them, and re-layouts: 5.43 us -> none  [the longest x1 3.51 us: shards(): doc_all = doc_ids[order_all]]
    unnamed x19 -> x0, local copies, waits for them, and re-layouts: 3.74 us -> none
    dot_general x6 -> x0, matrix products: 2.63 us -> none  [the longest x2 0.91 us: dot_nt(): lax.dot_general(left, right, (((1,), (1,)), ((), ())), preferred_element_...]
    convert_element_type x7 -> x0, other arithmetic: 1.55 us -> none  [the longest x1 0.86 us: shards(): rotate_back(dk_rot, cosine, sine_tab).astype(jnp.bfloat16)]
    slice x3 -> x0, local copies, waits for them, and re-layouts: 1.28 us -> none  [the longest x1 0.84 us: shards(): grad_values = summed[:, HK * HD:].astype(jnp.bfloat16)]
  transfers between devices with their start and end apart: 1 -> 0, of which waited for: 1 -> 0; matrix products, arithmetic and copies ran while one was open for 5% -> 0% of each run, Pallas kernels for 0% -> 0%
where the time goes in v1:
time: 17 us; the launch traced here: 16.8 us
  Pallas kernels  16.2 us (95%)
  between operations  0.64 us (4%)
    pallas_call x1, Pallas kernels, shards(): pl.pallas_call(functools.partial(kernel, n), out_shape=tuple((pltpu.VMEM(...  15.4 us
    pallas_call x1, Pallas kernels, shards(): pl.pallas_call(write_out, out_shape=tuple((jax.ShapeDtypeStruct(shape, BF...  0.79 us

profile of v1, /device:TPU:0, one launch (start us, length us, event | category | flops | bytes accessed | tf_op | source)
XLA Modules:
  0.0 16.8 jit_solution(131984853077467569)
XLA Ops:
  0.6 15.4 %shard_map.102 = (bf16[128,768]{1,0:T(8,128)(2,1)S(1)}, bf16[128,768]{1,0:T(8,128)(2,1)S(1)}, bf16[128,128]{1,0:T(8,128)(2,1)S(1)}, bf16[128,128]{1,0:T(8,128)(2,1)S(1)}) custom-call(s32[8]{0:T(128)} %order_ref.1, bf16[128,768]{1,0:T(8,128)(2,1)} %q_hbm.1, bf16[128,128]{1,0:T(8,128)(2,1)} %k_hbm.1, bf16[128,128]{1,0:T(8,128)(2,1)} %v_hbm.1, ...), custom_call_target="tpu_custom_call" | custom-call | tf_op jit(solution)/shard_map/pallas_call | solution.py:308
  16.0 0.8 %shard_map.103 = (bf16[128,768]{1,0:T(8,128)(2,1)}, bf16[128,768]{1,0:T(8,128)(2,1)}, bf16[128,128]{1,0:T(8,128)(2,1)}, bf16[128,128]{1,0:T(8,128)(2,1)}) custom-call(bf16[128,768]{1,0:T(8,128)(2,1)S(1)} %get-tuple-element.8.a, bf16[128,768]{1,0:T(8,128)(2,1)S(1)} %get-tuple-element.9.b, bf16[128,128]{1,0:T(8,128)(2,1)S(1)} %get-tuple-element.10.c, ...), custom_call_target="tpu_custom_call" | custom-call | tf_op jit(solution)/shard_map/pallas_call | solution.py:339

commit v2 on v1

--- a/solution.py
+++ b/solution.py
@@ -57,7 +57,7 @@
 def kernel(n, order_ref, q_hbm, k_hbm, v_hbm, do_hbm, pos_hbm, doc_hbm,
            out_ref, gq_ref, gk_ref, gv_ref,
            q_in, do_in, pos_in, doc_in, k_all, v_all, feat, lay, seqtab, q_rot, do_st, krot,
-           cos_t, sin_t, s_buf, dp_buf, p_buf, ds_buf, send_buf, recv_buf,
+           cos_t, sin_t, tops, s_buf, dp_buf, p_buf, ds_buf, send_buf, recv_buf,
            in_sem, ks_sem, kr_sem, vs_sem, vr_sem, gs_sem, gr_sem):
     me = lax.axis_index("cp")
     rows = k_hbm.shape[0]
@@ -175,64 +175,64 @@
         q_rot[h * rows:(h + 1) * rows, :] = (x * cosine + turned(x) * sine).astype(BF16)
         do_st[h * rows:(h + 1) * rows, :] = do_in[:, h * HD:(h + 1) * HD]
 
-    def chunk(c, tab, cc, ss, top):
+    factor = scale * math.log2(math.e)
+
+    def scores(c, tab, cc, ss):
         allowed = (tab[:, HD:] == doc_r) & (places(c, r_idx) <= orig_r)
         bias = jnp.where(allowed, 0.0, NEG)
         x = k_all[span(c), :].astype(F32)
         kr = (x * cc + turned(x) * ss).astype(BF16)
         krot[span(c), :] = kr
         sc = nt(kr, q_rot[...])
-        tops = []
+        peaks, sums = [], []
         for h in range(HQ):
-            part = sc[:, h * HD:(h + 1) * HD] + bias
-            s_buf[span(c), h * HD:(h + 1) * HD] = part
-            tops.append(jnp.max(part, axis=0, keepdims=True))
-        return jnp.maximum(top, jnp.concatenate(tops, axis=1))
+            cols = slice(h * rows, (h + 1) * rows)
+            part = sc[:, cols] + bias
+            top = jnp.max(part, axis=0, keepdims=True)
+            p = jnp.exp2((part - top) * factor)
+            s_buf[span(c), cols] = p
+            peaks.append(top)
+            sums.append(jnp.sum(p, axis=0, keepdims=True))
+        return jnp.concatenate(peaks, axis=1), jnp.concatenate(sums, axis=1)
 
     def grads(c):
-        dp_buf[span(c), :] = nt(v_all[span(c), :], do_st[...])
-
-    top = jnp.full((1, HQ * rows), NEG, F32)
-    top = chunk(me, own, cosine, sine, top)
-    grads(me)
-
-    def arrive(i, top):
+        dp = nt(v_all[span(c), :], do_st[...])
+        dp_buf[span(c), :] = dp
+        return jnp.sum(s_buf[span(c), :] * dp, axis=0, keepdims=True)
+
+    def merge(c, carry, top, total, weighted):
+        m, l, d = carry
+        tops[pl.ds(c, 1), :] = top
+        new = jnp.maximum(m, top)
+        old_w = jnp.exp2((m - new) * factor)
+        new_w = jnp.exp2((top - new) * factor)
+        return new, l * old_w + total * new_w, d * old_w + weighted * new_w
+
+    top, total = scores(me, own, cosine, sine)
+    weighted = grads(me)
+    tops[pl.ds(me, 1), :] = top
+    carry = (top, total, weighted)
+
+    def arrive(i, carry):
         c = frm(i)
         tab = blocks(c)
         cc, ss = tables(tab[:, :HD])
         kcopy(i).wait_recv()
-        top = chunk(c, tab, cc, ss, top)
+        top, total = scores(c, tab, cc, ss)
         vcopy(i).wait_recv()
-        grads(c)
-        return top
+        return merge(c, carry, top, total, grads(c))
 
     if small:
         for i in range(1, n):
-            top = arrive(i, top)
+            carry = arrive(i, carry)
     else:
-        top = lax.fori_loop(1, n, arrive, top)
-
-    factor = scale * math.log2(math.e)
-
-    def soft(c, carry):
-        total_p, total_d = carry
-        p = jnp.exp2((s_buf[span(c), :] - top) * factor)
-        s_buf[span(c), :] = p
-        return (total_p + jnp.sum(p, axis=0, keepdims=True),
-                total_d + jnp.sum(p * dp_buf[span(c), :], axis=0, keepdims=True))
-
-    zero = jnp.zeros((1, HQ * rows), F32)
-    carry = (zero, zero)
-    if small:
-        for c in range(n):
-            carry = soft(c, carry)
-    else:
-        carry = lax.fori_loop(0, n, soft, carry)
-    inv = 1.0 / carry[0]
-    delta = carry[1] * inv
+        carry = lax.fori_loop(1, n, arrive, carry)
+    inv = 1.0 / carry[1]
+    delta = carry[2] * inv
 
     def back(c):
-        probs = s_buf[span(c), :] * inv
+        share = jnp.exp2((tops[pl.ds(c, 1), :] - carry[0]) * factor) * inv
+        probs = s_buf[span(c), :] * share
         pb = probs.astype(BF16)
         db = (probs * (dp_buf[span(c), :] - delta)).astype(BF16)
         p_buf[span(c), :] = pb
@@ -325,6 +325,7 @@
             pltpu.VMEM((total, HD), BF16),
             pltpu.VMEM((rows, HD), F32),
             pltpu.VMEM((rows, HD), F32),
+            pltpu.VMEM((n, HQ * rows), F32),
             pltpu.VMEM((total, HQ * rows), F32),
             pltpu.VMEM((total, HQ * rows), F32),
             pltpu.VMEM((total, HQ * rows), BF16),

time: 17 us -> 16.7 us (0.982)
  Pallas kernels: 16.2 us -> 15.9 us
    pallas_call x1, Pallas kernels: 15.4 us -> 15.1 us  [shards(): pl.pallas_call(functools.partial(kernel, n), out_shape=tuple((pltpu.VMEM(...]
where the time goes in v2:
time: 16.7 us; the launch traced here: 16.6 us
  Pallas kernels  15.9 us (95%)
  between operations  0.64 us (4%)
    pallas_call x1, Pallas kernels, shards(): pl.pallas_call(functools.partial(kernel, n), out_shape=tuple((pltpu.VMEM(...  15.1 us
    pallas_call x1, Pallas kernels, shards(): pl.pallas_call(write_out, out_shape=tuple((jax.ShapeDtypeStruct(shape, BF...  0.79 us

profile of v2, /device:TPU:0, one launch (start us, length us, event | category | flops | bytes accessed | tf_op | source)
XLA Modules:
  0.0 16.6 jit_solution(4105528845763284333)
XLA Ops:
  0.6 15.1 %shard_map.102 = (bf16[128,768]{1,0:T(8,128)(2,1)S(1)}, bf16[128,768]{1,0:T(8,128)(2,1)S(1)}, bf16[128,128]{1,0:T(8,128)(2,1)S(1)}, bf16[128,128]{1,0:T(8,128)(2,1)S(1)}) custom-call(s32[8]{0:T(128)} %order_ref.1, bf16[128,768]{1,0:T(8,128)(2,1)} %q_hbm.1, bf16[128,128]{1,0:T(8,128)(2,1)} %k_hbm.1, bf16[128,128]{1,0:T(8,128)(2,1)} %v_hbm.1, ...), custom_call_target="tpu_custom_call" | custom-call | tf_op jit(solution)/shard_map/pallas_call | solution.py:308
  15.8 0.8 %shard_map.103 = (bf16[128,768]{1,0:T(8,128)(2,1)}, bf16[128,768]{1,0:T(8,128)(2,1)}, bf16[128,128]{1,0:T(8,128)(2,1)}, bf16[128,128]{1,0:T(8,128)(2,1)}) custom-call(bf16[128,768]{1,0:T(8,128)(2,1)S(1)} %get-tuple-element.8.a, bf16[128,768]{1,0:T(8,128)(2,1)S(1)} %get-tuple-element.9.b, bf16[128,128]{1,0:T(8,128)(2,1)S(1)} %get-tuple-element.10.c, ...), custom_call_target="tpu_custom_call" | custom-call | tf_op jit(solution)/shard_map/pallas_call | solution.py:340

commit v3 on v2

--- a/solution.py
+++ b/solution.py
@@ -57,8 +57,9 @@
 def kernel(n, order_ref, q_hbm, k_hbm, v_hbm, do_hbm, pos_hbm, doc_hbm,
            out_ref, gq_ref, gk_ref, gv_ref,
            q_in, do_in, pos_in, doc_in, k_all, v_all, feat, lay, seqtab, q_rot, do_st, krot,
-           cos_t, sin_t, tops, s_buf, dp_buf, p_buf, ds_buf, send_buf, recv_buf,
-           in_sem, ks_sem, kr_sem, vs_sem, vr_sem, gs_sem, gr_sem):
+           cos_t, sin_t, bias_t, tops, s_buf, dp_buf, p_buf, ds_buf, send_v, recv_v, send_k, recv_k,
+           in_sem, ks_sem, kr_sem, vs_sem, vr_sem,
+           gvs_sem, gvr_sem, gks_sem, gkr_sem):
     me = lax.axis_index("cp")
     rows = k_hbm.shape[0]
     total = rows * n
@@ -140,9 +141,6 @@
 
     first = lax.broadcasted_iota(jnp.int32, (rows, HD), 1) < HD // 2
 
-    def blocks(c):
-        return seqtab[span(c), :]
-
     def tables(turns):
         both = cos_turns(jnp.where(first, turns, turns - 0.25))
         other = pltpu.roll(both, HD // 2, 1)
@@ -151,10 +149,6 @@
     def turned(x):
         return pltpu.roll(x, HD // 2, 1)
 
-    own = blocks(me)
-    cosine, sine = tables(own[:, :HD])
-    cos_t[...] = cosine
-    sin_t[...] = sine
     r_idx = lax.broadcasted_iota(jnp.int32, (rows, HD), 0)
     l_idx = lax.broadcasted_iota(jnp.int32, (rows, HD), 1)
     doc_r = lay[3:4, mine]
@@ -168,8 +162,20 @@
 
     orig_r = places(me, l_idx)
 
+    def prepare(c):
+        tab = seqtab[span(c), :]
+        cosine, sine = tables(tab[:, :HD])
+        cos_t[span(c), :] = cosine
+        sin_t[span(c), :] = sine
+        allowed = (tab[:, HD:] == doc_r) & (places(c, r_idx) <= orig_r)
+        bias_t[span(c), :] = jnp.where(allowed, 0.0, NEG)
+
+    repeat(n, small, prepare)
+
     loads[4].wait()
     loads[5].wait()
+    cosine = cos_t[mine, :]
+    sine = sin_t[mine, :]
     for h in range(HQ):
         x = q_in[:, h * HD:(h + 1) * HD].astype(F32)
         q_rot[h * rows:(h + 1) * rows, :] = (x * cosine + turned(x) * sine).astype(BF16)
@@ -177,13 +183,12 @@
 
     factor = scale * math.log2(math.e)
 
-    def scores(c, tab, cc, ss):
-        allowed = (tab[:, HD:] == doc_r) & (places(c, r_idx) <= orig_r)
-        bias = jnp.where(allowed, 0.0, NEG)
+    def scores(c):
         x = k_all[span(c), :].astype(F32)
-        kr = (x * cc + turned(x) * ss).astype(BF16)
+        kr = (x * cos_t[span(c), :] + turned(x) * sin_t[span(c), :]).astype(BF16)
         krot[span(c), :] = kr
         sc = nt(kr, q_rot[...])
+        bias = bias_t[span(c), :]
         peaks, sums = [], []
         for h in range(HQ):
             cols = slice(h * rows, (h + 1) * rows)
@@ -193,66 +198,79 @@
             s_buf[span(c), cols] = p
             peaks.append(top)
             sums.append(jnp.sum(p, axis=0, keepdims=True))
-        return jnp.concatenate(peaks, axis=1), jnp.concatenate(sums, axis=1)
-
-    def grads(c):
-        dp = nt(v_all[span(c), :], do_st[...])
-        dp_buf[span(c), :] = dp
-        return jnp.sum(s_buf[span(c), :] * dp, axis=0, keepdims=True)
-
-    def merge(c, carry, top, total, weighted):
-        m, l, d = carry
+        top = jnp.concatenate(peaks, axis=1)
         tops[pl.ds(c, 1), :] = top
-        new = jnp.maximum(m, top)
-        old_w = jnp.exp2((m - new) * factor)
-        new_w = jnp.exp2((top - new) * factor)
-        return new, l * old_w + total * new_w, d * old_w + weighted * new_w
-
-    top, total = scores(me, own, cosine, sine)
-    weighted = grads(me)
-    tops[pl.ds(me, 1), :] = top
-    carry = (top, total, weighted)
+        return top, jnp.concatenate(sums, axis=1)
 
     def arrive(i, carry):
         c = frm(i)
-        tab = blocks(c)
-        cc, ss = tables(tab[:, :HD])
         kcopy(i).wait_recv()
-        top, total = scores(c, tab, cc, ss)
-        vcopy(i).wait_recv()
-        return merge(c, carry, top, total, grads(c))
-
+        m, l = carry
+        top, total = scores(c)
+        new = jnp.maximum(m, top)
+        return new, l * jnp.exp2((m - new) * factor) + total * jnp.exp2((top - new) * factor)
+
+    carry = scores(me)
+    dp_buf[mine, :] = nt(v_all[mine, :], do_st[...])
     if small:
         for i in range(1, n):
             carry = arrive(i, carry)
     else:
         carry = lax.fori_loop(1, n, arrive, carry)
+    top = carry[0]
     inv = 1.0 / carry[1]
-    delta = carry[2] * inv
-
-    def back(c):
-        share = jnp.exp2((tops[pl.ds(c, 1), :] - carry[0]) * factor) * inv
-        probs = s_buf[span(c), :] * share
+
+    def value_grad(c):
+        probs = s_buf[span(c), :] * (jnp.exp2((tops[pl.ds(c, 1), :] - top) * factor) * inv)
         pb = probs.astype(BF16)
-        db = (probs * (dp_buf[span(c), :] - delta)).astype(BF16)
+        s_buf[span(c), :] = probs
         p_buf[span(c), :] = pb
+        return nn(pb, do_st[...])
+
+    def gvcopy(i):
+        return pltpu.make_async_remote_copy(
+            src_ref=send_v.at[i - 1], dst_ref=recv_v.at[i - 1], send_sem=gvs_sem.at[i],
+            recv_sem=gvr_sem.at[i], device_id={"cp": to(i)}, device_id_type=pl.DeviceIdType.MESH)
+
+    def gkcopy(i):
+        return pltpu.make_async_remote_copy(
+            src_ref=send_k.at[i - 1], dst_ref=recv_k.at[i - 1], send_sem=gks_sem.at[i],
+            recv_sem=gkr_sem.at[i], device_id={"cp": to(i)}, device_id_type=pl.DeviceIdType.MESH)
+
+    def give_v(j):
+        i = n - 1 - j
+        send_v[i - 1, :, :] = value_grad(to(i)).astype(BF16)
+        gvcopy(i).start()
+
+    repeat(n - 1, small, give_v)
+    dv = value_grad(me)
+    delta = jnp.sum(s_buf[mine, :] * dp_buf[mine, :], axis=0, keepdims=True)
+
+    def weigh(i, delta):
+        c = frm(i)
+        vcopy(i).wait_recv()
+        dp = nt(v_all[span(c), :], do_st[...])
+        dp_buf[span(c), :] = dp
+        return delta + jnp.sum(s_buf[span(c), :] * dp, axis=0, keepdims=True)
+
+    if small:
+        for i in range(1, n):
+            delta = weigh(i, delta)
+    else:
+        delta = lax.fori_loop(1, n, weigh, delta)
+
+    def key_grad(c):
+        db = (s_buf[span(c), :] * (dp_buf[span(c), :] - delta)).astype(BF16)
         ds_buf[span(c), :] = db
-        return nn(db, q_rot[...]) * scale, nn(pb, do_st[...])
-
-    def gcopy(i):
-        return pltpu.make_async_remote_copy(
-            src_ref=send_buf.at[i - 1], dst_ref=recv_buf.at[i - 1], send_sem=gs_sem.at[i],
-            recv_sem=gr_sem.at[i], device_id={"cp": to(i)}, device_id_type=pl.DeviceIdType.MESH)
-
-    def give(j):
+        return nn(db, q_rot[...]) * scale
+
+    def give_k(j):
         i = n - 1 - j
-        dk, dv = back(to(i))
-        send_buf[i - 1, :, :HD] = dk.astype(BF16)
-        send_buf[i - 1, :, HD:] = dv.astype(BF16)
-        gcopy(i).start()
-
-    repeat(n - 1, small, give)
-    dk, dv = back(me)
+        send_k[i - 1, :, :] = key_grad(to(i)).astype(BF16)
+        gkcopy(i).start()
+
+    repeat(n - 1, small, give_k)
+    dk = key_grad(me)
 
     outt = lax.dot_general(v_all[...], p_buf[...], (((0,), (0,)), ((), ())),
                            preferred_element_type=F32)
@@ -262,25 +280,32 @@
         cols = slice(h * HD, (h + 1) * HD)
         out_ref[:, cols] = jnp.transpose(outt[:, h * rows:(h + 1) * rows]).astype(BF16)
         y = jnp.transpose(dqt[:, h * rows:(h + 1) * rows])
-        gq_ref[:, cols] = (y * cos_t[...] - turned(y) * sin_t[...]).astype(BF16)
-
-    def take(i, carry):
-        gcopy(i).wait_recv()
-        return (carry[0] + recv_buf[i - 1, :, :HD].astype(F32),
-                carry[1] + recv_buf[i - 1, :, HD:].astype(F32))
+        gq_ref[:, cols] = (y * cosine - turned(y) * sine).astype(BF16)
+
+    def take_v(i, dv):
+        gvcopy(i).wait_recv()
+        return dv + recv_v[i - 1, :, :].astype(F32)
+
+    def take_k(i, dk):
+        gkcopy(i).wait_recv()
+        return dk + recv_k[i - 1, :, :].astype(F32)
 
     if small:
         for i in range(1, n):
-            dk, dv = take(i, (dk, dv))
+            dv = take_v(i, dv)
+        gv_ref[...] = dv.astype(BF16)
+        for i in range(1, n):
+            dk = take_k(i, dk)
     else:
-        dk, dv = lax.fori_loop(1, n, take, (dk, dv))
-    gk_ref[...] = (dk * cos_t[...] - turned(dk) * sin_t[...]).astype(BF16)
-    gv_ref[...] = dv.astype(BF16)
+        gv_ref[...] = lax.fori_loop(1, n, take_v, dv).astype(BF16)
+        dk = lax.fori_loop(1, n, take_k, dk)
+    gk_ref[...] = (dk * cosine - turned(dk) * sine).astype(BF16)
 
     def finish(j):
         kcopy(j + 1).wait_send()
         vcopy(j + 1).wait_send()
-        gcopy(j + 1).wait_send()
+        gvcopy(j + 1).wait_send()
+        gkcopy(j + 1).wait_send()
 
     repeat(n - 1, small, finish)
 
@@ -323,17 +348,20 @@
             pltpu.VMEM((HQ * rows, HD), BF16),
             pltpu.VMEM((HQ * rows, HD), BF16),
             pltpu.VMEM((total, HD), BF16),
-            pltpu.VMEM((rows, HD), F32),
-            pltpu.VMEM((rows, HD), F32),
+            pltpu.VMEM((total, HD), F32),
+            pltpu.VMEM((total, HD), F32),
+            pltpu.VMEM((total, rows), F32),
             pltpu.VMEM((n, HQ * rows), F32),
             pltpu.VMEM((total, HQ * rows), F32),
             pltpu.VMEM((total, HQ * rows), F32),
             pltpu.VMEM((total, HQ * rows), BF16),
             pltpu.VMEM((total, HQ * rows), BF16),
-            pltpu.VMEM((n - 1, rows, 2 * HD), BF16),
-            pltpu.VMEM((n - 1, rows, 2 * HD), BF16),
+            pltpu.VMEM((n - 1, rows, HD), BF16),
+            pltpu.VMEM((n - 1, rows, HD), BF16),
+            pltpu.VMEM((n - 1, rows, HD), BF16),
+            pltpu.VMEM((n - 1, rows, HD), BF16),
             dma((6,)),
-            dma((n,)), dma((n,)), dma((n,)), dma((n,)), dma((n,)), dma((n,)),
+            dma((n,)), dma((n,)), dma((n,)), dma((n,)), dma((n,)), dma((n,)), dma((n,)), dma((n,)),
         ],
         compiler_params=pltpu.CompilerParams(collective_id=0, has_side_effects=True),
     )(stretch_order, queries, keys, values, out_grad, positions, doc_ids[None, :])

time: 16.7 us -> 16.5 us (0.988)
  Pallas kernels: 15.9 us -> 15.7 us
    pallas_call x1, Pallas kernels: 15.1 us -> 14.9 us  [shards(): pl.pallas_call(functools.partial(kernel, n), out_shape=tuple((pltpu.VMEM(...]
where the time goes in v3:
time: 16.5 us; the launch traced here: 16.3 us
  Pallas kernels  15.7 us (95%)
  between operations  0.64 us (4%)
    pallas_call x1, Pallas kernels, shards(): pl.pallas_call(functools.partial(kernel, n), out_shape=tuple((pltpu.VMEM(...  14.9 us
    pallas_call x1, Pallas kernels, shards(): pl.pallas_call(write_out, out_shape=tuple((jax.ShapeDtypeStruct(shape, BF...  0.79 us

profile of v3, /device:TPU:0, one launch (start us, length us, event | category | flops | bytes accessed | tf_op | source)
XLA Modules:
  0.0 16.3 jit_solution(12798826034109617711)
XLA Ops:
  0.6 14.9 %shard_map.102 = (bf16[128,768]{1,0:T(8,128)(2,1)S(1)}, bf16[128,768]{1,0:T(8,128)(2,1)S(1)}, bf16[128,128]{1,0:T(8,128)(2,1)S(1)}, bf16[128,128]{1,0:T(8,128)(2,1)S(1)}) custom-call(s32[8]{0:T(128)} %order_ref.1, bf16[128,768]{1,0:T(8,128)(2,1)} %q_hbm.1, bf16[128,128]{1,0:T(8,128)(2,1)} %k_hbm.1, bf16[128,128]{1,0:T(8,128)(2,1)} %v_hbm.1, ...), custom_call_target="tpu_custom_call" | custom-call | tf_op jit(solution)/shard_map/pallas_call | solution.py:333
  15.5 0.8 %shard_map.103 = (bf16[128,768]{1,0:T(8,128)(2,1)}, bf16[128,768]{1,0:T(8,128)(2,1)}, bf16[128,128]{1,0:T(8,128)(2,1)}, bf16[128,128]{1,0:T(8,128)(2,1)}) custom-call(bf16[128,768]{1,0:T(8,128)(2,1)S(1)} %get-tuple-element.8.a, bf16[128,768]{1,0:T(8,128)(2,1)S(1)} %get-tuple-element.9.b, bf16[128,128]{1,0:T(8,128)(2,1)S(1)} %get-tuple-element.10.c, ...), custom_call_target="tpu_custom_call" | custom-call | tf_op jit(solution)/shard_map/pallas_call | solution.py:368

commit v4 on v3

--- a/solution.py
+++ b/solution.py
@@ -54,16 +54,16 @@
         lax.fori_loop(0, n, lambda i, c: (body(i), c)[1], 0)
 
 
-def kernel(n, order_ref, q_hbm, k_hbm, v_hbm, do_hbm, pos_hbm, doc_hbm,
+def kernel(n, order_hbm, q_hbm, k_hbm, v_hbm, do_hbm, pos_hbm, doc_hbm,
            out_ref, gq_ref, gk_ref, gv_ref,
-           q_in, do_in, pos_in, doc_in, k_all, v_all, feat, lay, seqtab, q_rot, do_st, krot,
+           order_ref, q_in, do_in, pos_in, doc_in, k_all, v_all, feat, lay, seqtab, q_rot, do_st, krot,
            cos_t, sin_t, bias_t, tops, s_buf, dp_buf, p_buf, ds_buf, send_v, recv_v, send_k, recv_k,
            in_sem, ks_sem, kr_sem, vs_sem, vr_sem,
            gvs_sem, gvr_sem, gks_sem, gkr_sem):
     me = lax.axis_index("cp")
     rows = k_hbm.shape[0]
     total = rows * n
-    stretch = total // order_ref.shape[0]
+    stretch = total // order_hbm.shape[0]
     per = rows // stretch
     small = n <= 4 and n & (n - 1) == 0
     scale = 1.0 / math.sqrt(HD)
@@ -78,22 +78,23 @@
     def span(c):
         return pl.ds(pl.multiple_of(c * rows, rows), rows)
 
+    barrier = pltpu.get_barrier_semaphore()
+
+    def greet(i):
+        pl.semaphore_signal(barrier, inc=1, device_id={"cp": to(n - 1 - i)},
+                            device_id_type=pl.DeviceIdType.MESH)
+
+    repeat(n - 1, small, greet)
+
     loads = [
         pltpu.make_async_copy(src, dst, in_sem.at[j])
         for j, (src, dst) in enumerate((
             (k_hbm, k_all.at[mine]), (v_hbm, v_all.at[mine]), (pos_hbm, pos_in),
-            (doc_hbm, doc_in), (q_hbm, q_in), (do_hbm, do_in)))
+            (doc_hbm, doc_in), (q_hbm, q_in), (do_hbm, do_in), (order_hbm, order_ref)))
     ]
     for cp in loads:
         cp.start()
 
-    barrier = pltpu.get_barrier_semaphore()
-
-    def greet(i):
-        pl.semaphore_signal(barrier, inc=1, device_id={"cp": to(i + 1)},
-                            device_id_type=pl.DeviceIdType.MESH)
-
-    repeat(n - 1, small, greet)
     loads[0].wait()
     loads[1].wait()
     pl.semaphore_wait(barrier, n - 1)
@@ -111,7 +112,7 @@
     repeat(n - 1, small, lambda i: kcopy(n - 1 - i).start())
     repeat(n - 1, small, lambda i: vcopy(n - 1 - i).start())
 
-    for j in (2, 3):
+    for j in (2, 3, 6):
         loads[j].wait()
     feat[...] = jnp.zeros_like(feat)
     feat[0:3, :] = pos_in[...].astype(F32)
@@ -333,9 +334,10 @@
     held = pl.pallas_call(
         functools.partial(kernel, n),
         out_shape=tuple(pltpu.VMEM(shape, BF16) for shape in shapes),
-        in_specs=[pl.BlockSpec(memory_space=pltpu.SMEM)] + [hbm] * 6,
+        in_specs=[hbm] * 7,
         out_specs=(vmem,) * 4,
         scratch_shapes=[
+            pltpu.SMEM(stretch_order.shape, jnp.int32),
             pltpu.VMEM((rows, wide), BF16),
             pltpu.VMEM((rows, wide), BF16),
             pltpu.VMEM((3, total), jnp.int32),
@@ -360,7 +362,7 @@
             pltpu.VMEM((n - 1, rows, HD), BF16),
             pltpu.VMEM((n - 1, rows, HD), BF16),
             pltpu.VMEM((n - 1, rows, HD), BF16),
-            dma((6,)),
+            dma((7,)),
             dma((n,)), dma((n,)), dma((n,)), dma((n,)), dma((n,)), dma((n,)), dma((n,)), dma((n,)),
         ],
         compiler_params=pltpu.CompilerParams(collective_id=0, has_side_effects=True),

time: 16.5 us -> 15.8 us (0.958)
  Pallas kernels: 15.7 us -> 15 us
    pallas_call x1, Pallas kernels: 14.9 us -> 14.2 us  [shards(): pl.pallas_call(functools.partial(kernel, n), out_shape=tuple((pltpu.VMEM(...]
where the time goes in v4:
time: 15.8 us; the launch traced here: 15.6 us
  Pallas kernels  15 us (95%)
  between operations  0.64 us (4%)
    pallas_call x1, Pallas kernels, shards(): pl.pallas_call(functools.partial(kernel, n), out_shape=tuple((pltpu.VMEM(...  14.2 us
    pallas_call x1, Pallas kernels, shards(): pl.pallas_call(write_out, out_shape=tuple((jax.ShapeDtypeStruct(shape, BF...  0.79 us

profile of v4, /device:TPU:0, one launch (start us, length us, event | category | flops | bytes accessed | tf_op | source)
XLA Modules:
  0.0 15.6 jit_solution(10686067910442076368)
XLA Ops:
  0.6 14.2 %shard_map.102 = (bf16[128,768]{1,0:T(8,128)(2,1)S(1)}, bf16[128,768]{1,0:T(8,128)(2,1)S(1)}, bf16[128,128]{1,0:T(8,128)(2,1)S(1)}, bf16[128,128]{1,0:T(8,128)(2,1)S(1)}) custom-call(s32[8]{0:T(128)} %order_hbm.1, bf16[128,768]{1,0:T(8,128)(2,1)} %q_hbm.1, bf16[128,128]{1,0:T(8,128)(2,1)} %k_hbm.1, bf16[128,128]{1,0:T(8,128)(2,1)} %v_hbm.1, ...), custom_call_target="tpu_custom_call" | custom-call | tf_op jit(solution)/shard_map/pallas_call | solution.py:334
  14.8 0.8 %shard_map.103 = (bf16[128,768]{1,0:T(8,128)(2,1)}, bf16[128,768]{1,0:T(8,128)(2,1)}, bf16[128,128]{1,0:T(8,128)(2,1)}, bf16[128,128]{1,0:T(8,128)(2,1)}) custom-call(bf16[128,768]{1,0:T(8,128)(2,1)S(1)} %get-tuple-element.8.a, bf16[128,768]{1,0:T(8,128)(2,1)S(1)} %get-tuple-element.9.b, bf16[128,128]{1,0:T(8,128)(2,1)S(1)} %get-tuple-element.10.c, ...), custom_call_target="tpu_custom_call" | custom-call | tf_op jit(solution)/shard_map/pallas_call | solution.py:370
